TPU v7x, 256 devices: a whole 4x4x8 slice. The times are simulated.
256 devices in a mesh: row: 32 (over x, z_lo, y), col: 8 (over z_hi, core).
Axes of the slice: x: 4, y: 4, z: 8 (z_hi: 4, z_lo: 2; z = z_hi * 2 + z_lo), core: 2. Of those that a mesh axis runs over, the one named last changes fastest.
Arguments:
- jacobian: float32 [2, 16384, 256], P(None, ('row', 'col')), may hold values from -0.25 to 0.25
Outputs:
- normal_tiles: float32 [32, 4, 8, 512, 512], P('row', None, 'col')
All inputs are finite; a program needn't handle non-finite values.
Results may differ from a plain program's by a relative error of at most 0.0003.
Values sent between devices are 32-bit elements; how exact they have to be, the bound alone decides.
A program may use at most 64 MiB of HBM per device.

v0:
```python
import jax
import jax.numpy as jnp
from jax import lax
from jax.sharding import Mesh
from jax.sharding import PartitionSpec as P

ROW_COL = ("row_0", "row_1", "row_2", "col")
ROW = ("row_0", "row_1", "row_2")


def from_partner(block, axis, distance):
    count = lax.axis_size(axis)
    route = []
    for low in range(count):
        high = low | 1 << distance
        if high != low and high < count:
            route += [(low, high), (high, low)]
    return lax.ppermute(block, axis, route)


def laid_out(pieces, dim):
    dims = list(pieces.shape[1:])
    dims[dim] *= pieces.shape[0]
    return jnp.moveaxis(pieces, 0, dim).reshape(dims)


def sent_to_all(array, axis):
    devices = lax.axis_size(axis)
    return lax.all_to_all(
        jnp.broadcast_to(array[None], (devices, *array.shape)), axis, 0, 0, tiled=True
    )


def gather_directly(array, axis, dim):
    return laid_out(sent_to_all(array, axis), dim)


def stacked_from(array, axes, sequence):
    pieces = array
    for k in sequence:
        pieces = lax.all_gather(pieces, axes[k])
    done = sequence[::-1]
    back = [done.index(k) for k in range(len(axes))]
    pieces = pieces.transpose(*back, *range(len(axes), pieces.ndim))
    return pieces.reshape(-1, *array.shape)


def whole_of(array, axes, sequence, dim):
    return laid_out(stacked_from(array, axes, sequence), dim)


def partner_rows(block, bit_number):
    return from_partner(block, ROW_COL, bit_number)


def body(jacobian):
    row_index = lax.axis_index(ROW)
    col_index = lax.axis_index("col")
    col_count = lax.axis_size("col")
    cycles = lax.axis_size(ROW) // col_count
    panel_count = jacobian.shape[0]
    width = jacobian.shape[2]
    own_tile = gather_directly(jacobian, "col", 1)
    tile_size = own_tile.shape[1]
    col_bits = col_count.bit_length() - 1
    low_row = row_index % col_count
    moved = jacobian
    for bit_number in range(col_bits):
        first = partner_rows(moved, bit_number)
        second = partner_rows(first, bit_number + col_bits)
        differ = low_row >> bit_number & 1 != col_index >> bit_number & 1
        moved = jnp.where(differ, second, moved)
    gathered = whole_of(moved, ROW, (1, 0, 2), 1)
    gathered = gathered.reshape(panel_count, cycles, tile_size, width)
    partners = [gathered[:, turn_index] for turn_index in range(cycles)]
    stacked = jnp.stack(partners, 1)
    blocks = jnp.einsum("pak,ptbk->tab", own_tile, stacked, precision=lax.Precision.HIGHEST)
    column_tile = col_index + col_count * jnp.arange(cycles, dtype=jnp.int32)
    keep_mask = column_tile <= row_index
    blocks = jnp.where(keep_mask[:, None, None], blocks, jnp.zeros_like(blocks))
    return blocks[None, :, None]


def solution(mesh):
    split = Mesh(
        mesh.devices.reshape(4, 2, 4, mesh.shape["col"]), ("row_0", "row_1", "row_2", "col")
    )
    in_specs = (P(None, ROW_COL, None),)
    out_specs = P(ROW, None, "col", None, None)
    return jax.shard_map(body, mesh=split, in_specs=in_specs, out_specs=out_specs, check_vma=False)
```

profile of v0, /device:TPU:38, one launch (start us, length us, event | category | flops | bytes accessed | tf_op | source)
XLA Modules:
  0.0 156.1 jit_solution(7088069403335378075)
XLA Ops:
  6.5 1.6 collective-permute-done
  8.1 1.6 %collective-permute-start.1 = (f32[2,64,256]{2,1,0:T(8,128)S(1)}, f32[2,64,256]{2,1,0:T(8,128)S(1)}, u32[]{:S(2)}, u32[]{:S(2)}) collective-permute-start(f32[2,64,256]{2,1,0:T(8,128)S(1)} %collective-permute-done), channel_id=1, source_target_pairs={{0,8},{8,0},{1,9},{9,1},{2,10},{10,2},{3,11},{11,3},{4,12},{12,4},... | collective-permute-start | bytes 393224 | tf_op jit(solution)/shard_map/ppermute | solution.py:18
  9.7 4.0 %collective-permute-done.1 = f32[2,64,256]{2,1,0:T(8,128)S(1)} collective-permute-done((f32[2,64,256]{2,1,0:T(8,128)S(1)}, f32[2,64,256]{2,1,0:T(8,128)S(1)}, u32[]{:S(2)}, u32[]{:S(2)}) %collective-permute-start.1) | collective-permute-done | bytes 131104 | tf_op jit(solution)/shard_map/ppermute | solution.py:18
  13.6 0.9 broadcast_select_fusion
  14.6 3.4 %collective-permute-start.2 = (f32[2,64,256]{2,1,0:T(8,128)S(1)}, f32[2,64,256]{2,1,0:T(8,128)S(1)}, u32[]{:S(2)}, u32[]{:S(2)}) collective-permute-start(f32[2,64,256]{2,1,0:T(8,128)S(1)} %broadcast_select_fusion), channel_id=1, source_target_pairs={{0,2},{2,0},{1,3},{3,1},{4,6},{6,4},{5,7},{7,5},{8,10},{10,8},{9,1... | collective-permute-start | bytes 393224 | tf_op jit(solution)/shard_map/ppermute | solution.py:18
  17.9 3.7 %collective-permute-done.2 = f32[2,64,256]{2,1,0:T(8,128)S(1)} collective-permute-done((f32[2,64,256]{2,1,0:T(8,128)S(1)}, f32[2,64,256]{2,1,0:T(8,128)S(1)}, u32[]{:S(2)}, u32[]{:S(2)}) %collective-permute-start.2) | collective-permute-done | bytes 131104 | tf_op jit(solution)/shard_map/ppermute | solution.py:18
  21.6 3.2 %collective-permute-start.3 = (f32[2,64,256]{2,1,0:T(8,128)S(1)}, f32[2,64,256]{2,1,0:T(8,128)S(1)}, u32[]{:S(2)}, u32[]{:S(2)}) collective-permute-start(f32[2,64,256]{2,1,0:T(8,128)S(1)} %collective-permute-done.2), channel_id=1, source_target_pairs={{0,16},{16,0},{1,17},{17,1},{2,18},{18,2},{3,19},{19,3},{4,20},{20... | collective-permute-start | bytes 393224 | tf_op jit(solution)/shard_map/ppermute | solution.py:18
  24.8 3.3 %collective-permute-done.3 = f32[2,64,256]{2,1,0:T(8,128)S(1)} collective-permute-done((f32[2,64,256]{2,1,0:T(8,128)S(1)}, f32[2,64,256]{2,1,0:T(8,128)S(1)}, u32[]{:S(2)}, u32[]{:S(2)}) %collective-permute-start.3) | collective-permute-done | bytes 131104 | tf_op jit(solution)/shard_map/ppermute | solution.py:18
  28.1 5.4 %collective-permute-start.4 = (f32[2,64,256]{2,1,0:T(8,128)S(1)}, f32[2,64,256]{2,1,0:T(8,128)S(1)}, u32[]{:S(2)}, u32[]{:S(2)}) collective-permute-start(f32[2,64,256]{2,1,0:T(8,128)S(1)} %broadcast_select_fusion.1), channel_id=1, source_target_pairs={{0,4},{4,0},{1,5},{5,1},{2,6},{6,2},{3,7},{7,3},{8,12},{12,8},{9,1... | collective-permute-start | bytes 393224 | tf_op jit(solution)/shard_map/ppermute | solution.py:18
  33.5 3.7 %collective-permute-done.4 = f32[2,64,256]{2,1,0:T(8,128)S(1)} collective-permute-done((f32[2,64,256]{2,1,0:T(8,128)S(1)}, f32[2,64,256]{2,1,0:T(8,128)S(1)}, u32[]{:S(2)}, u32[]{:S(2)}) %collective-permute-start.4) | collective-permute-done | bytes 131104 | tf_op jit(solution)/shard_map/ppermute | solution.py:18
  37.2 1.8 %collective-permute-start.5 = (f32[2,64,256]{2,1,0:T(8,128)S(1)}, f32[2,64,256]{2,1,0:T(8,128)S(1)}, u32[]{:S(2)}, u32[]{:S(2)}) collective-permute-start(f32[2,64,256]{2,1,0:T(8,128)S(1)} %collective-permute-done.4), channel_id=1, source_target_pairs={{0,32},{32,0},{1,33},{33,1},{2,34},{34,2},{3,35},{35,3},{4,36},{36... | collective-permute-start | bytes 393224 | tf_op jit(solution)/shard_map/ppermute | solution.py:18
  39.0 3.2 %collective-permute-done.5 = f32[2,64,256]{2,1,0:T(8,128)S(1)} collective-permute-done((f32[2,64,256]{2,1,0:T(8,128)S(1)}, f32[2,64,256]{2,1,0:T(8,128)S(1)}, u32[]{:S(2)}, u32[]{:S(2)}) %collective-permute-start.5) | collective-permute-done | bytes 131104 | tf_op jit(solution)/shard_map/ppermute | solution.py:18
  42.2 5.7 %all-gather = f32[4,64,256]{2,1,0:T(8,128)} all-gather(f32[2,64,256]{2,1,0:T(8,128)S(1)} %broadcast_select_fusion.2), channel_id=2, replica_groups=mesh['row_0'=4,'row_1'=2,'row_2'=4,'col'=8] {'row_1'}, dimensions={0}, use_global_device_ids=true | all-gather | bytes 393216 | tf_op jit(solution)/shard_map/all_gather | solution.py:41
  48.0 0.0 all-gather.8.cloned.1.call-start
  48.0 30.6 %all-gather.6.cloned.1.call-done = f32[8,2,64,256]{3,2,1,0:T(8,128)} async-done(((f32[2,2,64,256]{3,2,1,0:T(8,128)}), f32[8,2,64,256]{3,2,1,0:T(8,128)}) %all-gather.6.cloned.1.call-update) | async-done | bytes 1048592 | tf_op jit(solution)/shard_map/all_gather | solution.py:41
  78.6 2.0 %broadcast_in_dim.22 = f32[8,2,64,256]{3,2,1,0:T(8,128)} broadcast(f32[2,64,256]{2,1,0:T(8,128)} %param.1), dimensions={1,2,3} | broadcast | bytes 1179648 | tf_op jit(solution)/shard_map/broadcast_in_dim | solution.py:30
  80.6 6.1 %all-to-all-start = ((f32[8,2,64,256]{3,2,1,0:T(8,128)}), f32[8,2,64,256]{3,2,1,0:T(8,128)S(1)}, u32[]{:S(2)}, u32[]{:S(2)}) async-start(f32[8,2,64,256]{3,2,1,0:T(8,128)} %broadcast_in_dim.22), calls=%async_computation | async-start | bytes 2097152 | tf_op jit(solution)/shard_map/all_to_all | solution.py:29
  86.7 29.5 %all-to-all-done = f32[8,2,64,256]{3,2,1,0:T(8,128)S(1)} async-done(((f32[8,2,64,256]{3,2,1,0:T(8,128)}), f32[8,2,64,256]{3,2,1,0:T(8,128)S(1)}, u32[]{:S(2)}, u32[]{:S(2)}) %all-to-all-start) | async-done | bytes 1048608 | tf_op jit(solution)/shard_map/all_to_all | solution.py:29
  116.2 0.1 copy.11
  116.3 16.5 %all-gather.8.cloned.1.call-done = f32[16,2,2,64,256]{4,3,2,1,0:T(8,128)} async-done(((f32[4,2,2,64,256]{4,3,2,1,0:T(8,128)}), f32[16,2,2,64,256]{4,3,2,1,0:T(8,128)}) %all-gather.8.cloned.1.call-update) | async-done | bytes 4194320 | tf_op jit(solution)/shard_map/all_gather | solution.py:41
  132.8 2.5 %copy.9 = f32[4,2,4,2,64,256]{5,4,3,2,1,0:T(8,128)S(1)} copy(f32[4,2,4,2,64,256]{5,4,3,1,0,2:T(8,128)} %bitcast.28) | data formatting | bytes 8388608 | tf_op jit(solution)/shard_map/transpose | solution.py:44
  135.2 0.5 copy.10
  135.7 8.3 %fusion = f32[1,4,1,512,512]{3,4,1,2,0:T(8,128)} fusion(f32[2,4,512,256]{3,2,1,0:T(8,128)S(1)} %bitcast.25, f32[2,512,256,1]{2,1,3,0:T(8,128)S(1)} %bitcast.27, pred[4]{0:T(512)(128)(4,1)S(1)} %add_compare_fusion), kind=kOutput, calls=%fused_computation.1 | convolution fusion | flops 6443499520 | bytes 9437188 | tf_op jit(solution)/shard_map/pak,ptbk->tab/dot_general | solution.py:77
  144.0 5.2 %copy.12 = f32[1,4,1,512,512]{4,3,2,1,0:T(8,128)} copy(f32[1,4,1,512,512]{3,4,1,2,0:T(8,128)} %fusion) | data formatting | bytes 8388608 | tf_op jit(solution)/shard_map/broadcast_in_dim | solution.py:81
  (7 shorter events, 0.1 us)
Async XLA Ops:
  6.5 72.1 %all-gather.6.cloned.1.call-start = ((), (), s32[]{:S(2)}) async-start(), calls=%async_computation.1 | async-start | bytes 1310720 | tf_op jit(solution)/shard_map/all_gather | solution.py:41
  6.5 1.6 collective-permute-start
  8.1 5.6 %collective-permute-start.1 = (f32[2,64,256]{2,1,0:T(8,128)S(1)}, f32[2,64,256]{2,1,0:T(8,128)S(1)}, u32[]{:S(2)}, u32[]{:S(2)}) collective-permute-start(f32[2,64,256]{2,1,0:T(8,128)S(1)} %collective-permute-done), channel_id=1, source_target_pairs={{0,8},{8,0},{1,9},{9,1},{2,10},{10,2},{3,11},{11,3},{4,12},{12,4},... | collective-permute-start | bytes 393224 | tf_op jit(solution)/shard_map/ppermute | solution.py:18
  14.6 7.0 %collective-permute-start.2 = (f32[2,64,256]{2,1,0:T(8,128)S(1)}, f32[2,64,256]{2,1,0:T(8,128)S(1)}, u32[]{:S(2)}, u32[]{:S(2)}) collective-permute-start(f32[2,64,256]{2,1,0:T(8,128)S(1)} %broadcast_select_fusion), channel_id=1, source_target_pairs={{0,2},{2,0},{1,3},{3,1},{4,6},{6,4},{5,7},{7,5},{8,10},{10,8},{9,1... | collective-permute-start | bytes 393224 | tf_op jit(solution)/shard_map/ppermute | solution.py:18
  21.6 6.5 %collective-permute-start.3 = (f32[2,64,256]{2,1,0:T(8,128)S(1)}, f32[2,64,256]{2,1,0:T(8,128)S(1)}, u32[]{:S(2)}, u32[]{:S(2)}) collective-permute-start(f32[2,64,256]{2,1,0:T(8,128)S(1)} %collective-permute-done.2), channel_id=1, source_target_pairs={{0,16},{16,0},{1,17},{17,1},{2,18},{18,2},{3,19},{19,3},{4,20},{20... | collective-permute-start | bytes 393224 | tf_op jit(solution)/shard_map/ppermute | solution.py:18
  28.1 9.1 %collective-permute-start.4 = (f32[2,64,256]{2,1,0:T(8,128)S(1)}, f32[2,64,256]{2,1,0:T(8,128)S(1)}, u32[]{:S(2)}, u32[]{:S(2)}) collective-permute-start(f32[2,64,256]{2,1,0:T(8,128)S(1)} %broadcast_select_fusion.1), channel_id=1, source_target_pairs={{0,4},{4,0},{1,5},{5,1},{2,6},{6,2},{3,7},{7,3},{8,12},{12,8},{9,1... | collective-permute-start | bytes 393224 | tf_op jit(solution)/shard_map/ppermute | solution.py:18
  37.2 5.0 %collective-permute-start.5 = (f32[2,64,256]{2,1,0:T(8,128)S(1)}, f32[2,64,256]{2,1,0:T(8,128)S(1)}, u32[]{:S(2)}, u32[]{:S(2)}) collective-permute-start(f32[2,64,256]{2,1,0:T(8,128)S(1)} %collective-permute-done.4), channel_id=1, source_target_pairs={{0,32},{32,0},{1,33},{33,1},{2,34},{34,2},{3,35},{35,3},{4,36},{36... | collective-permute-start | bytes 393224 | tf_op jit(solution)/shard_map/ppermute | solution.py:18
  48.0 84.8 %all-gather.8.cloned.1.call-start = ((), (), s32[]{:S(2)}) async-start(), calls=%async_computation.2 | async-start | bytes 5242880 | tf_op jit(solution)/shard_map/all_gather | solution.py:41
  80.6 35.6 %all-to-all-start = ((f32[8,2,64,256]{3,2,1,0:T(8,128)}), f32[8,2,64,256]{3,2,1,0:T(8,128)S(1)}, u32[]{:S(2)}, u32[]{:S(2)}) async-start(f32[8,2,64,256]{3,2,1,0:T(8,128)} %broadcast_in_dim.22), calls=%async_computation | async-start | bytes 2097152 | tf_op jit(solution)/shard_map/all_to_all | solution.py:29
Sparse Core Ops, SparseCore 0:
  48.1 30.4 all-gather.5
  80.4 52.3 all-gather.7
where the time goes:
time: 157 us; the launch traced here: 156 us
  waiting for transfers between devices  96 us (61%)
  starting transfers between devices  21.4 us (14%)
  between operations  13.4 us (9%)
  local copies, waits for them, and re-layouts  10.3 us (7%)
  matrix products  8.28 us (5%)
  blocking collectives  5.74 us (4%)
    all_gather x2, waiting for transfers between devices, stacked_from(): pieces = lax.all_gather(pieces, axes[k])  47 us
    all_to_all x1, waiting for transfers between devices, sent_to_all(): lax.all_to_all(jnp.broadcast_to(array[None], (devices, *array.shape)), ax...  29.5 us
    ppermute x6, waiting for transfers between devices, from_partner(): return lax.ppermute(block, axis, route)  19.4 us
    ppermute x6, starting transfers between devices, from_partner(): return lax.ppermute(block, axis, route)  15.3 us
    dot_general x1, matrix products, body(): jnp.einsum('pak,ptbk->tab', own_tile, stacked, precision=lax.Precision.HI...  8.28 us
    all_to_all x1, starting transfers between devices, sent_to_all(): lax.all_to_all(jnp.broadcast_to(array[None], (devices, *array.shape)), ax...  6.11 us
    all_gather x1, blocking collectives, stacked_from(): pieces = lax.all_gather(pieces, axes[k])  5.74 us
    broadcast_in_dim x1, local copies, waits for them, and re-layouts, body(): return blocks[None, :, None]  5.22 us
  transfers between devices with their start and end apart: 9, of which 9 were waited for; matrix products, arithmetic and copies ran while one was open for 1% of the time, Pallas kernels for 0%

commit v1 on v0

v1 whole, which is shorter than its diff:
```python
import jax
import jax.numpy as jnp
from jax import lax
from jax.experimental import pallas as pl
from jax.experimental.pallas import tpu as pltpu
from jax.sharding import PartitionSpec as P

NX, NL, NY, NH, NK = 4, 2, 4, 4, 2
QUARTERS = 4


def class_of(d):
    return ("x" if d in (0, 2) else "y"), (1 if d in (0, 1) else -1)


def hops(d, dt, ds):
    first, way = class_of(d)
    a, b = (dt, ds) if first == "x" else (ds, dt)
    second = "y" if first == "x" else "x"
    if b == 0:
        arrives = None if a == 0 else (first, -way if a == 2 else a)
        sends = []
        if a == 0:
            sends += [(first, 1), (first, -1)]
        elif a == -way:
            sends += [(first, way)]
        sends += [(second, 1), (second, -1)]
    else:
        arrives = (second, -way if b == 2 else b)
        sends = [(second, way)] if b == -way else []
    return arrives, sends


def distance(v):
    return abs(v)


def schedule():
    begin = {0: 0.0, 1: 2.0, 3: 2.0, 2: 4.0}
    order = []
    for d in range(NH):
        for dt in (0, 1, -1, 2):
            for ds in (0, 1, -1, 2):
                steps = distance(dt) + distance(ds)
                order.append((begin[d] + 3.0 * steps, d, dt, ds))
    order.sort(key=lambda e: e[0])
    return order


def mod(v, n):
    return lax.rem(v + 2 * n, n)


def kernel(jac_ref, out_ref, rows, cols, a_cat, b_cat, local_sem, dist_send, dist_recv, row_send, row_recv,
           core_send, core_recv, send_sem, recv_sem):
    row = lax.axis_index("row")
    col = lax.axis_index("col")
    x, l, y = row // 8, (row // 4) % 2, row % 4
    h, k = col // 2, col % 2
    tile = row % 8
    aim_h, aim_k = tile // 2, tile % 2
    from_l, from_y = col // 4, col % 4
    own_column = tile == col

    def device(x_, l_, y_, h_, k_):
        return ((x_ * NL + l_) * NY + y_, h_ * NK + k_)

    def neighbour(axis, way):
        if axis == "x":
            return device(mod(x + way, NX), l, y, h, k)
        if axis == "y":
            return device(x, l, mod(y + way, NY), h, k)
        if axis == "h":
            return device(x, l, y, mod(h + way, NH), k)
        return device(x, l, y, h, 1 - k)

    def remote(src, dst, send, recv, to):
        return pltpu.make_async_remote_copy(
            src_ref=src, dst_ref=dst, send_sem=send, recv_sem=recv, device_id=to,
            device_id_type=pl.DeviceIdType.MESH,
        )

    load = pltpu.make_async_copy(jac_ref, rows.at[col], local_sem.at[0])
    load.start()
    own = pltpu.make_async_copy(jac_ref.at[y], cols.at[x, h, y, k], local_sem.at[1])
    pl.when(own_column)(own.start)

    barrier = pltpu.get_barrier_semaphore()
    greet = [neighbour("x", 1), neighbour("x", -1), neighbour("y", 1), neighbour("y", -1),
             neighbour("h", 1), neighbour("h", -1), neighbour("k", 0)]
    for to in greet:
        pl.semaphore_signal(barrier, inc=1, device_id=to, device_id_type=pl.DeviceIdType.MESH)
    for e in range(NH * NK):
        def signal():
            pl.semaphore_signal(barrier, inc=1, device_id=device(x, from_l, from_y, e // NK, e % NK),
                                device_id_type=pl.DeviceIdType.MESH)
        pl.when((e != col) | jnp.logical_not(own_column))(signal)
    expected = len(greet) + NY * NL
    pl.when(own_column)(lambda: pl.semaphore_wait(barrier, expected - 1))
    pl.when(jnp.logical_not(own_column))(lambda: pl.semaphore_wait(barrier, expected))
    load.wait()

    finish = []

    def go(copy, cond=None):
        if cond is None:
            copy.start()
        else:
            pl.when(cond)(copy.start)
        finish.append((copy, cond))

    for s in range(QUARTERS):
        for l_ in range(NL):
            copy = remote(rows.at[col, s], cols.at[x, h, s, k], dist_send.at[s * NL + l_], dist_recv.at[h, k],
                          device(x, l_, s, aim_h, aim_k))
            mine = own_column & (y == s) & (l == l_)
            go(copy, jnp.logical_not(mine))
    for way in (1, -1):
        n = 0 if way == 1 else 1
        go(remote(rows.at[col], rows.at[col], row_send.at[n], row_recv.at[n], neighbour("h", way)))
    go(remote(rows.at[col], rows.at[col], core_send.at[0], core_recv.at[0], neighbour("k", 0)))

    def rows_arrive(n):
        if n < 2:
            way = 1 if n == 0 else -1
            piece = mod(h - way, NH) * NK + k
            remote(rows.at[piece], rows.at[piece], row_send.at[n], row_recv.at[n], neighbour("h", way)).wait_recv()
            half = rows.at[piece, pl.ds(2 * n, 2)]
            go(remote(half, half, row_send.at[2 + n], row_recv.at[2 + n], neighbour("h", way)))
        else:
            piece = mod(h + 2, NH) * NK + k
            for m in range(2):
                half = rows.at[piece, pl.ds(2 * m, 2)]
                remote(half, half, row_send.at[2 + m], row_recv.at[2 + m], neighbour("h", 1)).wait_recv()
        go(remote(rows.at[piece], rows.at[piece], core_send.at[1 + n], core_recv.at[1 + n], neighbour("k", 0)))

    def cores_arrive():
        for n, dh in enumerate((0, -1, 1, 2)):
            piece = mod(h + dh, NH) * NK + 1 - k
            remote(rows.at[piece], rows.at[piece], core_send.at[n], core_recv.at[n], neighbour("k", 0)).wait_recv()
        for piece in range(NH * NK):
            for s in range(QUARTERS):
                split(rows[piece, s], a_cat, slice(64 * piece + 32 * (s % 2), 64 * piece + 32 * (s % 2) + 32),
                      s // 2, True)

    def split(values, target, at, panel, left):
        high = values.astype(jnp.bfloat16)
        low = (values - high.astype(jnp.float32)).astype(jnp.bfloat16)
        parts = (high, high, low) if left else (high, low, high)
        for n, part in enumerate(parts):
            target[at, 512 * n + 256 * panel : 512 * n + 256 * panel + 256] = part

    counter = [0]

    def there(t, way, plane):
        keeps = plane >= t
        return keeps if way == 1 else keeps | ((t == 1) & (plane == 0))

    def chunk_copy(t, h_, s, n, to):
        chunk = cols.at[t, h_, s]
        return remote(chunk, chunk, send_sem.at[n], recv_sem.at[t, h_, s], to)

    def arrive(d, dt, ds):
        t, h_, s = mod(x + dt, NX), mod(h + d, NH), mod(y + ds, NY)
        first, way = class_of(d)
        came, sends = hops(d, dt, ds)
        here = there(t, way, x)
        passing = None if dt != 0 else True

        def wait():
            if came is None:
                for k_ in range(NK):
                    landed = remote(rows.at[0, 0], cols.at[t, h_, s, k_], dist_send.at[0], dist_recv.at[h_, k_],
                                    neighbour("k", 0))
                    if d == 0:
                        mine = own_column & (k == k_)
                        pl.when(mine)(own.wait)
                        pl.when(jnp.logical_not(mine))(landed.wait_recv)
                    else:
                        landed.wait_recv()
            else:
                chunk_copy(t, h_, s, 0, neighbour("x", 1)).wait_recv()

        if came is None:
            wait()
        elif came[0] == "y":
            if dt == 0:
                wait()
            else:
                pl.when(x > t)(wait)
        else:
            pl.when(here)(wait)
        for axis, step in sends:
            n = counter[0]
            counter[0] += 1
            copy = chunk_copy(t, h_, s, n, neighbour(axis, step))
            if axis == "x":
                go(copy, here & there(t, way, mod(x + step, NX)))
            elif dt == 0:
                go(copy)
            else:
                go(copy, x > t)

    def compute(dt):
        t = mod(x + dt, NX)
        wanted = (t < x) | ((t == x) & (col <= tile))

        def products():
            for h_ in range(NH):
                for s in range(QUARTERS):
                    for k_ in range(NK):
                        at = 128 * h_ + 64 * k_ + 32 * (s % 2)
                        split(cols[t, h_, s, k_], b_cat, slice(at, at + 32), s // 2, False)
            for n in range(2):
                out_ref[0, t, 0, :, 256 * n : 256 * n + 256] = lax.dot_general(
                    a_cat[...], b_cat[256 * n : 256 * n + 256, :], (((1,), (1,)), ((), ())),
                    preferred_element_type=jnp.float32)

        def nothing():
            out_ref[0, t, 0] = jnp.zeros(out_ref.shape[3:], jnp.float32)

        pl.when(wanted)(products)
        pl.when(jnp.logical_not(wanted))(nothing)

    events = [(time, ("chunk", d, dt, ds)) for time, d, dt, ds in schedule()]
    events += [(9.0, ("rows", 0)), (9.0, ("rows", 1)), (12.2, ("rows", 2)), (13.1, ("cores",))]
    events.sort(key=lambda e: e[0])
    for _, event in events:
        if event[0] == "chunk":
            arrive(*event[1:])
        elif event[0] == "rows":
            rows_arrive(event[1])
        else:
            cores_arrive()
    for dt in (0, 1, -1, 2):
        compute(dt)
    for copy, cond in finish:
        if cond is None:
            copy.wait_send()
        else:
            pl.when(cond)(copy.wait_send)


def count_sends():
    return sum(len(hops(d, dt, ds)[1]) for _, d, dt, ds in schedule())


def body(jacobian):
    quarters = jacobian.reshape(QUARTERS, 32, 256)
    dma = pltpu.SemaphoreType.DMA
    return pl.pallas_call(
        kernel,
        out_shape=pltpu.VMEM((1, NX, 1, 512, 512), jnp.float32),
        in_specs=[pl.BlockSpec(memory_space=pltpu.HBM)],
        out_specs=pl.BlockSpec(memory_space=pltpu.VMEM),
        scratch_shapes=[
            pltpu.VMEM((NH * NK, QUARTERS, 32, 256), jnp.float32),
            pltpu.VMEM((NX, NH, QUARTERS, NK, 32, 256), jnp.float32),
            pltpu.VMEM((512, 1536), jnp.bfloat16),
            pltpu.VMEM((512, 1536), jnp.bfloat16),
            dma((2,)),
            dma((QUARTERS * NL,)),
            dma((NH, NK)),
            dma((4,)),
            dma((4,)),
            dma((4,)),
            dma((4,)),
            dma((count_sends(),)),
            dma((NX, NH, QUARTERS)),
        ],
        compiler_params=pltpu.CompilerParams(collective_id=0, has_side_effects=True, vmem_limit_bytes=40 << 20),
    )(quarters)


def solution(mesh):
    return jax.shard_map(
        body, mesh=mesh, in_specs=(P(None, ("row", "col"), None),), out_specs=P("row", None, "col", None, None),
        check_vma=False,
    )
```

time: 157 us -> 56 us (0.36)
  the two profiles are of different devices: /device:TPU:38 before, /device:TPU:54 now
where the time goes in v1:
time: 56 us; the launch traced here: 55.9 us
  Pallas kernels  52.9 us (94%)
  local copies, waits for them, and re-layouts  2.92 us (5%)
    pallas_call x1, Pallas kernels, body(): pl.pallas_call(kernel, out_shape=pltpu.VMEM((1, NX, 1, 512, 512), jnp.flo...  52.9 us
    unnamed x3, local copies, waits for them, and re-layouts  2.92 us

profile of v1, /device:TPU:54, one launch (start us, length us, event | category | flops | bytes accessed | tf_op | source)
XLA Modules:
  0.0 55.9 jit_solution(13740976234011136818)
XLA Ops:
  0.0 0.0 copy-start
  0.0 0.9 %copy-done = f32[2,64,256]{2,1,0:T(8,128)S(1)} copy-done((f32[2,64,256]{2,1,0:T(8,128)S(1)}, f32[2,64,256]{2,1,0:T(8,128)}, u32[]{:S(2)}) %copy-start) | copy-done | bytes 131096
  0.9 52.9 %shard_map.17 = f32[1,4,1,512,512]{4,3,2,1,0:T(8,128)S(1)} custom-call(f32[4,32,256]{2,1,0:T(8,128)S(1)} %bitcast.1), custom_call_target="tpu_custom_call" | custom-call | tf_op jit(solution)/shard_map/pallas_call | solution.py:251
  53.9 2.0 %copy.3 = f32[1,4,1,512,512]{4,3,2,1,0:T(8,128)} copy(f32[1,4,1,512,512]{4,3,2,1,0:T(8,128)S(1)} %shard_map.17) | data formatting | bytes 8388608
Async XLA Ops:
  0.0 0.9 %copy-start = (f32[2,64,256]{2,1,0:T(8,128)S(1)}, f32[2,64,256]{2,1,0:T(8,128)}, u32[]{:S(2)}) copy-start(f32[2,64,256]{2,1,0:T(8,128)} %param.1) | copy-start | bytes 393220

commit v2 on v1

--- a/solution.py
+++ b/solution.py
@@ -7,6 +7,7 @@
 
 NX, NL, NY, NH, NK = 4, 2, 4, 4, 2
 QUARTERS = 4
+VMEM = 62800000
 
 
 def class_of(d):
@@ -31,20 +32,20 @@
     return arrives, sends
 
 
-def distance(v):
-    return abs(v)
-
-
-def schedule():
-    begin = {0: 0.0, 1: 2.0, 3: 2.0, 2: 4.0}
-    order = []
-    for d in range(NH):
-        for dt in (0, 1, -1, 2):
-            for ds in (0, 1, -1, 2):
-                steps = distance(dt) + distance(ds)
-                order.append((begin[d] + 3.0 * steps, d, dt, ds))
-    order.sort(key=lambda e: e[0])
-    return order
+ORDER = (
+    (0, 0, 0, 0), (0, 1, 0, 0), (0, 3, 0, 0), (0, 0, -1, 0), (0, 2, 0, 0), (0, 1, 0, -1), (0, 3, 0, 1),
+    (0, 2, 1, 0), (0, 3, 1, 0), (0, 1, 0, 1), (2, 0), (0, 0, 2, 0), (0, 0, 1, 0), (0, 0, -1, 1), (0, 0, 0, -1),
+    (0, 1, -1, -1), (0, 3, 0, -1), (0, 2, -1, 0), (0, 2, 0, 1), (0, 0, 2, 1), (0, 1, 0, 2), (0, 0, -1, -1),
+    (0, 3, 0, 2), (0, 1, 1, 1), (0, 0, 0, 1), (0, 0, 1, -1), (0, 0, 2, -1), (0, 1, -1, 1), (0, 3, -1, 0),
+    (0, 2, 2, 0), (0, 3, 1, 1), (2, 1), (0, 2, 0, -1), (0, 3, 1, -1), (0, 2, -1, 1), (0, 2, 1, 1), (2, 2),
+    (0, 0, 0, 2), (0, 3, -1, -1), (0, 2, 0, 2), (3,), (0, 1, -1, 0), (1, 0, 0), (0, 3, 2, 0), (0, 0, 1, 1),
+    (1, 0, 1), (0, 3, -1, 1), (0, 2, 2, 1), (0, 3, 1, 2), (0, 1, -1, 2), (0, 2, -1, -1), (0, 1, 2, 1),
+    (0, 1, 1, 0), (0, 1, 1, -1), (0, 0, -1, 2), (0, 1, 2, -1), (1, -1, 0), (0, 0, 1, 2), (0, 2, 1, -1),
+    (0, 1, 1, 2), (0, 2, -1, 2), (0, 3, -1, 2), (1, 1, 0), (0, 3, 2, 1), (0, 1, 2, 0), (1, -1, 1), (0, 0, 2, 2),
+    (0, 2, 1, 2), (1, 1, 1), (0, 3, 2, -1), (0, 1, 2, 2), (1, 2, 0), (0, 2, 2, -1), (0, 2, 2, 2), (0, 3, 2, 2),
+    (1, 2, 1),
+)
+PAIRS = ((0, 1), (3, 2))
 
 
 def mod(v, n):
@@ -95,6 +96,14 @@
             pl.semaphore_signal(barrier, inc=1, device_id=device(x, from_l, from_y, e // NK, e % NK),
                                 device_id_type=pl.DeviceIdType.MESH)
         pl.when((e != col) | jnp.logical_not(own_column))(signal)
+    def wanted(t):
+        return (t < x) | ((t == x) & (col <= tile))
+
+    for t in range(NX):
+        def nothing():
+            out_ref[0, t, 0] = jnp.zeros(out_ref.shape[3:], jnp.float32)
+        pl.when(jnp.logical_not(wanted(t)))(nothing)
+
     expected = len(greet) + NY * NL
     pl.when(own_column)(lambda: pl.semaphore_wait(barrier, expected - 1))
     pl.when(jnp.logical_not(own_column))(lambda: pl.semaphore_wait(barrier, expected))
@@ -201,39 +210,33 @@
             else:
                 go(copy, x > t)
 
-    def compute(dt):
+    def compute(dt, pair):
         t = mod(x + dt, NX)
-        wanted = (t < x) | ((t == x) & (col <= tile))
 
         def products():
-            for h_ in range(NH):
+            for m, d in enumerate(PAIRS[pair]):
+                h_ = mod(h + d, NH)
                 for s in range(QUARTERS):
                     for k_ in range(NK):
-                        at = 128 * h_ + 64 * k_ + 32 * (s % 2)
+                        at = 128 * m + 64 * k_ + 32 * (s % 2)
                         split(cols[t, h_, s, k_], b_cat, slice(at, at + 32), s // 2, False)
-            for n in range(2):
-                out_ref[0, t, 0, :, 256 * n : 256 * n + 256] = lax.dot_general(
-                    a_cat[...], b_cat[256 * n : 256 * n + 256, :], (((1,), (1,)), ((), ())),
-                    preferred_element_type=jnp.float32)
-
-        def nothing():
-            out_ref[0, t, 0] = jnp.zeros(out_ref.shape[3:], jnp.float32)
-
-        pl.when(wanted)(products)
-        pl.when(jnp.logical_not(wanted))(nothing)
-
-    events = [(time, ("chunk", d, dt, ds)) for time, d, dt, ds in schedule()]
-    events += [(9.0, ("rows", 0)), (9.0, ("rows", 1)), (12.2, ("rows", 2)), (13.1, ("cores",))]
-    events.sort(key=lambda e: e[0])
-    for _, event in events:
-        if event[0] == "chunk":
+            block = lax.dot_general(
+                a_cat[...], b_cat[...], (((1,), (1,)), ((), ())), preferred_element_type=jnp.float32)
+            for m, d in enumerate(PAIRS[pair]):
+                at = pl.multiple_of(128 * mod(h + d, NH), 128)
+                out_ref[0, t, 0, :, pl.ds(at, 128)] = block[:, 128 * m : 128 * m + 128]
+
+        pl.when(wanted(t))(products)
+
+    for event in ORDER:
+        if event[0] == 0:
             arrive(*event[1:])
-        elif event[0] == "rows":
+        elif event[0] == 1:
+            compute(*event[1:])
+        elif event[0] == 2:
             rows_arrive(event[1])
         else:
             cores_arrive()
-    for dt in (0, 1, -1, 2):
-        compute(dt)
     for copy, cond in finish:
         if cond is None:
             copy.wait_send()
@@ -242,7 +245,7 @@
 
 
 def count_sends():
-    return sum(len(hops(d, dt, ds)[1]) for _, d, dt, ds in schedule())
+    return sum(len(hops(*event[1:])[1]) for event in ORDER if event[0] == 0)
 
 
 def body(jacobian):
@@ -257,7 +260,7 @@
             pltpu.VMEM((NH * NK, QUARTERS, 32, 256), jnp.float32),
             pltpu.VMEM((NX, NH, QUARTERS, NK, 32, 256), jnp.float32),
             pltpu.VMEM((512, 1536), jnp.bfloat16),
-            pltpu.VMEM((512, 1536), jnp.bfloat16),
+            pltpu.VMEM((256, 1536), jnp.bfloat16),
             dma((2,)),
             dma((QUARTERS * NL,)),
             dma((NH, NK)),
@@ -268,7 +271,7 @@
             dma((count_sends(),)),
             dma((NX, NH, QUARTERS)),
         ],
-        compiler_params=pltpu.CompilerParams(collective_id=0, has_side_effects=True, vmem_limit_bytes=40 << 20),
+        compiler_params=pltpu.CompilerParams(collective_id=0, has_side_effects=True, vmem_limit_bytes=VMEM),
     )(quarters)
 
 

time: 56 us -> 49.7 us (0.89)
  the two profiles are of different devices: /device:TPU:54 before, /device:TPU:69 now
where the time goes in v2:
time: 49.7 us
  Pallas kernels  47.7 us (96%)
  local copies, waits for them, and re-layouts  2.02 us (4%)
    pallas_call x1, Pallas kernels, body(): pl.pallas_call(kernel, out_shape=pltpu.VMEM((1, NX, 1, 512, 512), jnp.flo...  47.7 us
    unnamed x1, local copies, waits for them, and re-layouts  2.02 us

profile of v2, /device:TPU:69, one launch (start us, length us, event | category | flops | bytes accessed | tf_op | source)
XLA Modules:
  0.0 49.7 jit_solution(3678923274385624758)
XLA Ops:
  0.0 47.7 %shard_map.17 = f32[1,4,1,512,512]{4,3,2,1,0:T(8,128)S(1)} custom-call(f32[4,32,256]{2,1,0:T(8,128)} %bitcast.1), custom_call_target="tpu_custom_call" | custom-call | tf_op jit(solution)/shard_map/pallas_call | solution.py:254
  47.7 2.0 %copy.3 = f32[1,4,1,512,512]{4,3,2,1,0:T(8,128)} copy(f32[1,4,1,512,512]{4,3,2,1,0:T(8,128)S(1)} %shard_map.17) | data formatting | bytes 8388608

commit v3 on v2

--- a/solution.py
+++ b/solution.py
@@ -33,17 +33,16 @@
 
 
 ORDER = (
-    (0, 0, 0, 0), (0, 1, 0, 0), (0, 3, 0, 0), (0, 0, -1, 0), (0, 2, 0, 0), (0, 1, 0, -1), (0, 3, 0, 1),
-    (0, 2, 1, 0), (0, 3, 1, 0), (0, 1, 0, 1), (2, 0), (0, 0, 2, 0), (0, 0, 1, 0), (0, 0, -1, 1), (0, 0, 0, -1),
-    (0, 1, -1, -1), (0, 3, 0, -1), (0, 2, -1, 0), (0, 2, 0, 1), (0, 0, 2, 1), (0, 1, 0, 2), (0, 0, -1, -1),
-    (0, 3, 0, 2), (0, 1, 1, 1), (0, 0, 0, 1), (0, 0, 1, -1), (0, 0, 2, -1), (0, 1, -1, 1), (0, 3, -1, 0),
-    (0, 2, 2, 0), (0, 3, 1, 1), (2, 1), (0, 2, 0, -1), (0, 3, 1, -1), (0, 2, -1, 1), (0, 2, 1, 1), (2, 2),
-    (0, 0, 0, 2), (0, 3, -1, -1), (0, 2, 0, 2), (3,), (0, 1, -1, 0), (1, 0, 0), (0, 3, 2, 0), (0, 0, 1, 1),
-    (1, 0, 1), (0, 3, -1, 1), (0, 2, 2, 1), (0, 3, 1, 2), (0, 1, -1, 2), (0, 2, -1, -1), (0, 1, 2, 1),
-    (0, 1, 1, 0), (0, 1, 1, -1), (0, 0, -1, 2), (0, 1, 2, -1), (1, -1, 0), (0, 0, 1, 2), (0, 2, 1, -1),
-    (0, 1, 1, 2), (0, 2, -1, 2), (0, 3, -1, 2), (1, 1, 0), (0, 3, 2, 1), (0, 1, 2, 0), (1, -1, 1), (0, 0, 2, 2),
-    (0, 2, 1, 2), (1, 1, 1), (0, 3, 2, -1), (0, 1, 2, 2), (1, 2, 0), (0, 2, 2, -1), (0, 2, 2, 2), (0, 3, 2, 2),
-    (1, 2, 1),
+    (0, 0, 0, 0), (0, 0, 1, 0), (0, 0, -1, 0), (0, 1, 0, 0), (0, 3, 0, 0), (0, 2, 0, 0), (0, 1, 1, 0),
+    (0, 0, -1, 1), (2, 0), (0, 1, 0, 1), (0, 0, 0, -1), (2, 1), (0, 3, 0, 1), (0, 1, -1, 0), (0, 3, 0, -1),
+    (0, 2, -1, 0), (0, 2, 1, 0), (0, 1, 0, -1), (0, 3, -1, 0), (0, 0, 2, 0), (0, 2, 0, 1), (0, 0, 1, -1),
+    (0, 1, -1, 1), (0, 3, 0, 2), (0, 2, -1, 1), (0, 2, 0, -1), (0, 2, 2, 0), (0, 3, 1, 1), (0, 3, 1, 0), (2, 2),
+    (0, 2, 1, 1), (0, 0, -1, -1), (0, 3, -1, 1), (0, 0, 0, 1), (0, 2, 1, -1), (0, 0, 0, 2), (0, 3, -1, -1),
+    (3,), (0, 3, 1, -1), (0, 2, 0, 2), (0, 0, 1, 1), (0, 2, -1, -1), (0, 1, 0, 2), (0, 0, 2, -1), (0, 2, -1, 2),
+    (0, 1, 1, -1), (0, 0, 2, 1), (1, 0, 0), (1, 0, 1), (0, 3, 1, 2), (0, 2, 2, 1), (0, 2, 2, -1), (0, 1, 2, 0),
+    (0, 1, -1, -1), (0, 0, 1, 2), (0, 3, -1, 2), (0, 2, 1, 2), (0, 3, 2, 1), (0, 0, -1, 2), (0, 1, 2, 1),
+    (1, -1, 1), (0, 1, 1, 1), (0, 1, -1, 2), (0, 3, 2, 0), (0, 1, 2, -1), (1, 1, 1), (1, -1, 0), (0, 1, 1, 2),
+    (0, 0, 2, 2), (0, 2, 2, 2), (1, 1, 0), (0, 3, 2, -1), (0, 1, 2, 2), (1, 2, 0), (0, 3, 2, 2), (1, 2, 1),
 )
 PAIRS = ((0, 1), (3, 2))
 
@@ -52,16 +51,14 @@
     return lax.rem(v + 2 * n, n)
 
 
-def kernel(jac_ref, out_ref, rows, cols, a_cat, b_cat, local_sem, dist_send, dist_recv, row_send, row_recv,
-           core_send, core_recv, send_sem, recv_sem):
+def kernel(jac_ref, out_ref, rows, lines, cols, a_cat, b_cat, local_sem, line_send, line_recv, dist_send, dist_recv,
+           row_send, row_recv, core_send, core_recv, send_sem, recv_sem):
     row = lax.axis_index("row")
     col = lax.axis_index("col")
     x, l, y = row // 8, (row // 4) % 2, row % 4
     h, k = col // 2, col % 2
     tile = row % 8
-    aim_h, aim_k = tile // 2, tile % 2
-    from_l, from_y = col // 4, col % 4
-    own_column = tile == col
+    from_l = col // 4
 
     def device(x_, l_, y_, h_, k_):
         return ((x_ * NL + l_) * NY + y_, h_ * NK + k_)
@@ -83,19 +80,17 @@
 
     load = pltpu.make_async_copy(jac_ref, rows.at[col], local_sem.at[0])
     load.start()
-    own = pltpu.make_async_copy(jac_ref.at[y], cols.at[x, h, y, k], local_sem.at[1])
-    pl.when(own_column)(own.start)
-
     barrier = pltpu.get_barrier_semaphore()
     greet = [neighbour("x", 1), neighbour("x", -1), neighbour("y", 1), neighbour("y", -1),
+             neighbour("y", 2),
              neighbour("h", 1), neighbour("h", -1), neighbour("k", 0)]
     for to in greet:
         pl.semaphore_signal(barrier, inc=1, device_id=to, device_id_type=pl.DeviceIdType.MESH)
     for e in range(NH * NK):
         def signal():
-            pl.semaphore_signal(barrier, inc=1, device_id=device(x, from_l, from_y, e // NK, e % NK),
+            pl.semaphore_signal(barrier, inc=1, device_id=device(x, from_l, y, e // NK, e % NK),
                                 device_id_type=pl.DeviceIdType.MESH)
-        pl.when((e != col) | jnp.logical_not(own_column))(signal)
+        pl.when((e != col) | (l != from_l))(signal)
     def wanted(t):
         return (t < x) | ((t == x) & (col <= tile))
 
@@ -104,9 +99,9 @@
             out_ref[0, t, 0] = jnp.zeros(out_ref.shape[3:], jnp.float32)
         pl.when(jnp.logical_not(wanted(t)))(nothing)
 
-    expected = len(greet) + NY * NL
-    pl.when(own_column)(lambda: pl.semaphore_wait(barrier, expected - 1))
-    pl.when(jnp.logical_not(own_column))(lambda: pl.semaphore_wait(barrier, expected))
+    expected = len(greet) + NH * NK
+    pl.when(l == from_l)(lambda: pl.semaphore_wait(barrier, expected - 1))
+    pl.when(l != from_l)(lambda: pl.semaphore_wait(barrier, expected))
     load.wait()
 
     finish = []
@@ -118,12 +113,30 @@
             pl.when(cond)(copy.start)
         finish.append((copy, cond))
 
-    for s in range(QUARTERS):
+    def crossing(dy):
+        copy = remote(rows.at[col, mod(y + dy, NY)], lines.at[y], line_send.at[dy % NY - 1],
+                      line_recv.at[dy % NY - 1], neighbour("y", dy))
+        return copy
+
+    for dy in (1, -1, 2):
+        go(crossing(dy))
+    for dy in (0, 1, -1, 2):
+        line = mod(y + dy, NY)
+        if dy == 0:
+            quarter = rows.at[col, y]
+        else:
+            quarter = lines.at[line]
+            remote(rows.at[col, y], quarter, line_send.at[-dy % NY - 1], line_recv.at[-dy % NY - 1],
+                   neighbour("y", dy)).wait_recv()
+        aim_h, aim_k = 2 * l + line // 2, line % 2
         for l_ in range(NL):
-            copy = remote(rows.at[col, s], cols.at[x, h, s, k], dist_send.at[s * NL + l_], dist_recv.at[h, k],
-                          device(x, l_, s, aim_h, aim_k))
-            mine = own_column & (y == s) & (l == l_)
+            to = cols.at[x, h, y, k]
+            mine = (aim_h == h) & (aim_k == k) & (l == l_)
+            copy = remote(quarter, to, dist_send.at[dy % NY * NL + l_], dist_recv.at[h, k],
+                          device(x, l_, y, aim_h, aim_k))
             go(copy, jnp.logical_not(mine))
+            stay = pltpu.make_async_copy(quarter, to, local_sem.at[1])
+            pl.when(mine)(stay.start)
     for way in (1, -1):
         n = 0 if way == 1 else 1
         go(remote(rows.at[col], rows.at[col], row_send.at[n], row_recv.at[n], neighbour("h", way)))
@@ -182,8 +195,8 @@
                     landed = remote(rows.at[0, 0], cols.at[t, h_, s, k_], dist_send.at[0], dist_recv.at[h_, k_],
                                     neighbour("k", 0))
                     if d == 0:
-                        mine = own_column & (k == k_)
-                        pl.when(mine)(own.wait)
+                        mine = (l == from_l) & (k == k_)
+                        pl.when(mine)(pltpu.make_async_copy(rows.at[0, 0], cols.at[t, h_, s, k_], local_sem.at[1]).wait)
                         pl.when(jnp.logical_not(mine))(landed.wait_recv)
                     else:
                         landed.wait_recv()
@@ -258,11 +271,14 @@
         out_specs=pl.BlockSpec(memory_space=pltpu.VMEM),
         scratch_shapes=[
             pltpu.VMEM((NH * NK, QUARTERS, 32, 256), jnp.float32),
+            pltpu.VMEM((NY, 32, 256), jnp.float32),
             pltpu.VMEM((NX, NH, QUARTERS, NK, 32, 256), jnp.float32),
             pltpu.VMEM((512, 1536), jnp.bfloat16),
             pltpu.VMEM((256, 1536), jnp.bfloat16),
             dma((2,)),
-            dma((QUARTERS * NL,)),
+            dma((NY - 1,)),
+            dma((NY - 1,)),
+            dma((NY * NL,)),
             dma((NH, NK)),
             dma((4,)),
             dma((4,)),

time: 49.7 us -> 46.1 us (0.928)
  the two profiles are of different devices: /device:TPU:69 before, /device:TPU:38 now
where the time goes in v3:
time: 46.1 us; the launch traced here: 46 us
  Pallas kernels  44 us (95%)
  local copies, waits for them, and re-layouts  2.02 us (4%)
    pallas_call x1, Pallas kernels, body(): pl.pallas_call(kernel, out_shape=pltpu.VMEM((1, NX, 1, 512, 512), jnp.flo...  44 us
    unnamed x1, local copies, waits for them, and re-layouts  2.02 us

profile of v3, /device:TPU:38, one launch (start us, length us, event | category | flops | bytes accessed | tf_op | source)
XLA Modules:
  0.0 46.0 jit_solution(13303179255084815529)
XLA Ops:
  0.0 44.0 %shard_map.17 = f32[1,4,1,512,512]{4,3,2,1,0:T(8,128)S(1)} custom-call(f32[4,32,256]{2,1,0:T(8,128)} %bitcast.1), custom_call_target="tpu_custom_call" | custom-call | tf_op jit(solution)/shard_map/pallas_call | solution.py:267
  44.0 2.0 %copy.3 = f32[1,4,1,512,512]{4,3,2,1,0:T(8,128)} copy(f32[1,4,1,512,512]{4,3,2,1,0:T(8,128)S(1)} %shard_map.17) | data formatting | bytes 8388608

commit v4 on v3

--- a/solution.py
+++ b/solution.py
@@ -7,7 +7,7 @@
 
 NX, NL, NY, NH, NK = 4, 2, 4, 4, 2
 QUARTERS = 4
-VMEM = 62800000
+VMEM = 56900000
 
 
 def class_of(d):
@@ -45,13 +45,69 @@
     (0, 0, 2, 2), (0, 2, 2, 2), (1, 1, 0), (0, 3, 2, -1), (0, 1, 2, 2), (1, 2, 0), (0, 3, 2, 2), (1, 2, 1),
 )
 PAIRS = ((0, 1), (3, 2))
+LATE = tuple(event[1:] for event in ORDER if event[0] == 1)[6:]
 
 
 def mod(v, n):
     return lax.rem(v + 2 * n, n)
 
 
-def kernel(jac_ref, out_ref, rows, lines, cols, a_cat, b_cat, local_sem, line_send, line_recv, dist_send, dist_recv,
+def split(values, target, at, panel, left):
+    high = values.astype(jnp.bfloat16)
+    low = (values - high.astype(jnp.float32)).astype(jnp.bfloat16)
+    parts = (high, high, low) if left else (high, low, high)
+    for n, part in enumerate(parts):
+        target[at, 512 * n + 256 * panel : 512 * n + 256 * panel + 256] = part
+
+
+def unit(cols, a_cat, b_cat, t, h, pair):
+    for m, d in enumerate(PAIRS[pair]):
+        h_ = mod(h + d, NH)
+        for s in range(QUARTERS):
+            for k_ in range(NK):
+                at = 128 * m + 64 * k_ + 32 * (s % 2)
+                split(cols[t, h_, s, k_], b_cat, slice(at, at + 32), s // 2, False)
+    return lax.dot_general(a_cat[...], b_cat[...], (((1,), (1,)), ((), ())), preferred_element_type=jnp.float32)
+
+
+def finish_tiles(tiles, a_cat, cols, out_ref, b_cat, late, sem):
+    row = lax.axis_index("row")
+    col = lax.axis_index("col")
+    x, h, tile = row // 8, col // 2, row % 8
+    finish = []
+
+    def put(source, dt, d):
+        t = mod(x + dt, NX)
+        block = pl.ds(pl.multiple_of(128 * mod(h + d, NH), 128), 128)
+        source = tiles.at[0, t, 0, :, block] if source is None else source
+        return pltpu.make_async_copy(source, out_ref.at[0, t, 0, :, block], sem.at[4 * (dt % NX) + d])
+
+    for dt in (0, 1, -1, 2):
+        for pair in range(2):
+            t = mod(x + dt, NX)
+            waits = ((t < x) | ((t == x) & (col <= tile))) if (dt, pair) in LATE else False
+            for d in PAIRS[pair]:
+                copy = put(None, dt, d)
+                if waits is False:
+                    copy.start()
+                else:
+                    pl.when(jnp.logical_not(waits))(copy.start)
+                finish.append(copy)
+    for n, (dt, pair) in enumerate(LATE):
+        t = mod(x + dt, NX)
+
+        def products():
+            block = unit(cols, a_cat, b_cat, t, h, pair)
+            for m, d in enumerate(PAIRS[pair]):
+                late[2 * n + m] = block[:, 128 * m : 128 * m + 128]
+                put(late.at[2 * n + m], dt, d).start()
+
+        pl.when((t < x) | ((t == x) & (col <= tile)))(products)
+    for copy in finish:
+        copy.wait()
+
+
+def kernel(jac_ref, out_ref, a_cat, cols, rows, lines, b_cat, local_sem, line_send, line_recv, dist_send, dist_recv,
            row_send, row_recv, core_send, core_recv, send_sem, recv_sem):
     row = lax.axis_index("row")
     col = lax.axis_index("col")
@@ -165,13 +221,6 @@
                 split(rows[piece, s], a_cat, slice(64 * piece + 32 * (s % 2), 64 * piece + 32 * (s % 2) + 32),
                       s // 2, True)
 
-    def split(values, target, at, panel, left):
-        high = values.astype(jnp.bfloat16)
-        low = (values - high.astype(jnp.float32)).astype(jnp.bfloat16)
-        parts = (high, high, low) if left else (high, low, high)
-        for n, part in enumerate(parts):
-            target[at, 512 * n + 256 * panel : 512 * n + 256 * panel + 256] = part
-
     counter = [0]
 
     def there(t, way, plane):
@@ -227,14 +276,7 @@
         t = mod(x + dt, NX)
 
         def products():
-            for m, d in enumerate(PAIRS[pair]):
-                h_ = mod(h + d, NH)
-                for s in range(QUARTERS):
-                    for k_ in range(NK):
-                        at = 128 * m + 64 * k_ + 32 * (s % 2)
-                        split(cols[t, h_, s, k_], b_cat, slice(at, at + 32), s // 2, False)
-            block = lax.dot_general(
-                a_cat[...], b_cat[...], (((1,), (1,)), ((), ())), preferred_element_type=jnp.float32)
+            block = unit(cols, a_cat, b_cat, t, h, pair)
             for m, d in enumerate(PAIRS[pair]):
                 at = pl.multiple_of(128 * mod(h + d, NH), 128)
                 out_ref[0, t, 0, :, pl.ds(at, 128)] = block[:, 128 * m : 128 * m + 128]
@@ -245,7 +287,8 @@
         if event[0] == 0:
             arrive(*event[1:])
         elif event[0] == 1:
-            compute(*event[1:])
+            if event[1:] not in LATE:
+                compute(*event[1:])
         elif event[0] == 2:
             rows_arrive(event[1])
         else:
@@ -264,16 +307,18 @@
 def body(jacobian):
     quarters = jacobian.reshape(QUARTERS, 32, 256)
     dma = pltpu.SemaphoreType.DMA
-    return pl.pallas_call(
+    tiles, rows_cat, cols = pl.pallas_call(
         kernel,
-        out_shape=pltpu.VMEM((1, NX, 1, 512, 512), jnp.float32),
+        out_shape=(
+            pltpu.VMEM((1, NX, 1, 512, 512), jnp.float32),
+            pltpu.VMEM((512, 1536), jnp.bfloat16),
+            pltpu.VMEM((NX, NH, QUARTERS, NK, 32, 256), jnp.float32),
+        ),
         in_specs=[pl.BlockSpec(memory_space=pltpu.HBM)],
-        out_specs=pl.BlockSpec(memory_space=pltpu.VMEM),
+        out_specs=(pl.BlockSpec(memory_space=pltpu.VMEM),) * 3,
         scratch_shapes=[
             pltpu.VMEM((NH * NK, QUARTERS, 32, 256), jnp.float32),
             pltpu.VMEM((NY, 32, 256), jnp.float32),
-            pltpu.VMEM((NX, NH, QUARTERS, NK, 32, 256), jnp.float32),
-            pltpu.VMEM((512, 1536), jnp.bfloat16),
             pltpu.VMEM((256, 1536), jnp.bfloat16),
             dma((2,)),
             dma((NY - 1,)),
@@ -289,6 +334,18 @@
         ],
         compiler_params=pltpu.CompilerParams(collective_id=0, has_side_effects=True, vmem_limit_bytes=VMEM),
     )(quarters)
+    return pl.pallas_call(
+        finish_tiles,
+        out_shape=jax.ShapeDtypeStruct((1, NX, 1, 512, 512), jnp.float32),
+        in_specs=[pl.BlockSpec(memory_space=pltpu.VMEM)] * 3,
+        out_specs=pl.BlockSpec(memory_space=pltpu.HBM),
+        scratch_shapes=[
+            pltpu.VMEM((256, 1536), jnp.bfloat16),
+            pltpu.VMEM((max(1, 2 * len(LATE)), 512, 128), jnp.float32),
+            dma((4 * NX,)),
+        ],
+        compiler_params=pltpu.CompilerParams(vmem_limit_bytes=8 << 20),
+    )(tiles, rows_cat, cols)
 
 
 def solution(mesh):

time: 46.1 us -> 45 us (0.976)
  local copies, waits for them, and re-layouts: 2.02 us -> 0 us
  Pallas kernels: 44 us -> 44.9 us
    unnamed x1 -> x0, local copies, waits for them, and re-layouts: 2.02 us -> none
    pallas_call x1 -> x2, Pallas kernels: 44 us -> 44.9 us  [the longest x1 42.7 us: body(): pl.pallas_call(kernel, out_shape=(pltpu.VMEM((1, NX, 1, 512, 512), jnp.fl...]
where the time goes in v4:
time: 45 us; the launch traced here: 44.9 us
  Pallas kernels  44.9 us (100%)
    pallas_call x1, Pallas kernels, body(): pl.pallas_call(kernel, out_shape=(pltpu.VMEM((1, NX, 1, 512, 512), jnp.fl...  42.7 us
    pallas_call x1, Pallas kernels, body(): pl.pallas_call(finish_tiles, out_shape=jax.ShapeDtypeStruct((1, NX, 1, 51...  2.2 us

profile of v4, /device:TPU:38, one launch (start us, length us, event | category | flops | bytes accessed | tf_op | source)
XLA Modules:
  0.0 44.9 jit_solution(13471793344516736116)
XLA Ops:
  0.0 42.7 %shard_map.17 = (f32[1,4,1,512,512]{4,3,2,1,0:T(8,128)S(1)}, bf16[512,1536]{1,0:T(8,128)(2,1)S(1)}, f32[4,4,4,2,32,256]{5,4,3,2,1,0:T(8,128)S(1)}) custom-call(f32[4,32,256]{2,1,0:T(8,128)} %bitcast.1), custom_call_target="tpu_custom_call" | custom-call | tf_op jit(solution)/shard_map/pallas_call | solution.py:310
  42.7 2.2 %shard_map.18 = f32[1,4,1,512,512]{4,3,2,1,0:T(8,128)} custom-call(f32[1,4,1,512,512]{4,3,2,1,0:T(8,128)S(1)} %get-tuple-element.8.tiles, bf16[512,1536]{1,0:T(8,128)(2,1)S(1)} %get-tuple-element.9.a_cat, f32[4,4,4,2,32,256]{5,4,3,2,1,0:T(8,128)S(1)} %get-tuple-element.10.cols), custom_call_target="tpu_custom_call" | custom-call | tf_op jit(solution)/shard_map/pallas_call | solution.py:337

commit v5 on v4

--- a/solution.py
+++ b/solution.py
@@ -37,12 +37,13 @@
     (0, 0, -1, 1), (2, 0), (0, 1, 0, 1), (0, 0, 0, -1), (2, 1), (0, 3, 0, 1), (0, 1, -1, 0), (0, 3, 0, -1),
     (0, 2, -1, 0), (0, 2, 1, 0), (0, 1, 0, -1), (0, 3, -1, 0), (0, 0, 2, 0), (0, 2, 0, 1), (0, 0, 1, -1),
     (0, 1, -1, 1), (0, 3, 0, 2), (0, 2, -1, 1), (0, 2, 0, -1), (0, 2, 2, 0), (0, 3, 1, 1), (0, 3, 1, 0), (2, 2),
-    (0, 2, 1, 1), (0, 0, -1, -1), (0, 3, -1, 1), (0, 0, 0, 1), (0, 2, 1, -1), (0, 0, 0, 2), (0, 3, -1, -1),
-    (3,), (0, 3, 1, -1), (0, 2, 0, 2), (0, 0, 1, 1), (0, 2, -1, -1), (0, 1, 0, 2), (0, 0, 2, -1), (0, 2, -1, 2),
-    (0, 1, 1, -1), (0, 0, 2, 1), (1, 0, 0), (1, 0, 1), (0, 3, 1, 2), (0, 2, 2, 1), (0, 2, 2, -1), (0, 1, 2, 0),
-    (0, 1, -1, -1), (0, 0, 1, 2), (0, 3, -1, 2), (0, 2, 1, 2), (0, 3, 2, 1), (0, 0, -1, 2), (0, 1, 2, 1),
-    (1, -1, 1), (0, 1, 1, 1), (0, 1, -1, 2), (0, 3, 2, 0), (0, 1, 2, -1), (1, 1, 1), (1, -1, 0), (0, 1, 1, 2),
-    (0, 0, 2, 2), (0, 2, 2, 2), (1, 1, 0), (0, 3, 2, -1), (0, 1, 2, 2), (1, 2, 0), (0, 3, 2, 2), (1, 2, 1),
+    (0, 2, 1, 1), (0, 0, -1, -1), (0, 3, -1, 1), (0, 0, 0, 1), (3,), (0, 2, 1, -1), (0, 0, 0, 2),
+    (0, 3, -1, -1), (0, 3, 1, -1), (0, 2, 0, 2), (0, 0, 1, 1), (0, 2, -1, -1), (0, 1, 0, 2), (0, 0, 2, -1),
+    (0, 2, -1, 2), (0, 1, 1, -1), (0, 0, 2, 1), (1, 0, 0), (1, 0, 1), (0, 3, 1, 2), (0, 2, 2, 1), (0, 2, 2, -1),
+    (0, 1, 2, 0), (0, 1, -1, -1), (0, 0, 1, 2), (0, 3, -1, 2), (0, 2, 1, 2), (0, 3, 2, 1), (0, 0, -1, 2),
+    (0, 1, 2, 1), (1, -1, 1), (0, 1, 1, 1), (0, 1, -1, 2), (0, 3, 2, 0), (0, 1, 2, -1), (1, 1, 1), (1, -1, 0),
+    (0, 1, 1, 2), (0, 0, 2, 2), (0, 2, 2, 2), (1, 1, 0), (0, 3, 2, -1), (0, 1, 2, 2), (1, 2, 0), (0, 3, 2, 2),
+    (1, 2, 1),
 )
 PAIRS = ((0, 1), (3, 2))
 LATE = tuple(event[1:] for event in ORDER if event[0] == 1)[6:]

time: 45 us -> 45 us (level)
  no operation moved by 1% of the time
where the time goes in v5:
time: 45 us; the launch traced here: 44.9 us
  Pallas kernels  44.9 us (100%)
    pallas_call x1, Pallas kernels, body(): pl.pallas_call(kernel, out_shape=(pltpu.VMEM((1, NX, 1, 512, 512), jnp.fl...  42.7 us
    pallas_call x1, Pallas kernels, body(): pl.pallas_call(finish_tiles, out_shape=jax.ShapeDtypeStruct((1, NX, 1, 51...  2.2 us

profile of v5, /device:TPU:38, one launch (start us, length us, event | category | flops | bytes accessed | tf_op | source)
XLA Modules:
  0.0 44.9 jit_solution(10764669975953744250)
XLA Ops:
  0.0 42.7 %shard_map.17 = (f32[1,4,1,512,512]{4,3,2,1,0:T(8,128)S(1)}, bf16[512,1536]{1,0:T(8,128)(2,1)S(1)}, f32[4,4,4,2,32,256]{5,4,3,2,1,0:T(8,128)S(1)}) custom-call(f32[4,32,256]{2,1,0:T(8,128)} %bitcast.1), custom_call_target="tpu_custom_call" | custom-call | tf_op jit(solution)/shard_map/pallas_call | solution.py:311
  42.7 2.2 %shard_map.18 = f32[1,4,1,512,512]{4,3,2,1,0:T(8,128)} custom-call(f32[1,4,1,512,512]{4,3,2,1,0:T(8,128)S(1)} %get-tuple-element.8.tiles, bf16[512,1536]{1,0:T(8,128)(2,1)S(1)} %get-tuple-element.9.a_cat, f32[4,4,4,2,32,256]{5,4,3,2,1,0:T(8,128)S(1)} %get-tuple-element.10.cols), custom_call_target="tpu_custom_call" | custom-call | tf_op jit(solution)/shard_map/pallas_call | solution.py:338

commit v6 on v5

--- a/solution.py
+++ b/solution.py
@@ -175,7 +175,7 @@
                       line_recv.at[dy % NY - 1], neighbour("y", dy))
         return copy
 
-    for dy in (1, -1, 2):
+    for dy in (2, 1, -1):
         go(crossing(dy))
     for dy in (0, 1, -1, 2):
         line = mod(y + dy, NY)

time: 45 us -> 45.5 us (1.011)
  Pallas kernels: 44.9 us -> 45.4 us
    pallas_call x1, Pallas kernels: 42.7 us -> 43.2 us  [body(): pl.pallas_call(kernel, out_shape=(pltpu.VMEM((1, NX, 1, 512, 512), jnp.fl...]
where the time goes in v6:
time: 45.5 us; the launch traced here: 45.4 us
  Pallas kernels  45.4 us (100%)
    pallas_call x1, Pallas kernels, body(): pl.pallas_call(kernel, out_shape=(pltpu.VMEM((1, NX, 1, 512, 512), jnp.fl...  43.2 us
    pallas_call x1, Pallas kernels, body(): pl.pallas_call(finish_tiles, out_shape=jax.ShapeDtypeStruct((1, NX, 1, 51...  2.2 us

profile of v6, /device:TPU:38, one launch (start us, length us, event | category | flops | bytes accessed | tf_op | source)
XLA Modules:
  0.0 45.4 jit_solution(6895522528361013687)
XLA Ops:
  0.0 43.2 %shard_map.17 = (f32[1,4,1,512,512]{4,3,2,1,0:T(8,128)S(1)}, bf16[512,1536]{1,0:T(8,128)(2,1)S(1)}, f32[4,4,4,2,32,256]{5,4,3,2,1,0:T(8,128)S(1)}) custom-call(f32[4,32,256]{2,1,0:T(8,128)} %bitcast.1), custom_call_target="tpu_custom_call" | custom-call | tf_op jit(solution)/shard_map/pallas_call | solution.py:311
  43.2 2.2 %shard_map.18 = f32[1,4,1,512,512]{4,3,2,1,0:T(8,128)} custom-call(f32[1,4,1,512,512]{4,3,2,1,0:T(8,128)S(1)} %get-tuple-element.8.tiles, bf16[512,1536]{1,0:T(8,128)(2,1)S(1)} %get-tuple-element.9.a_cat, f32[4,4,4,2,32,256]{5,4,3,2,1,0:T(8,128)S(1)} %get-tuple-element.10.cols), custom_call_target="tpu_custom_call" | custom-call | tf_op jit(solution)/shard_map/pallas_call | solution.py:338
